TPU v7x, 256 devices: a whole 4x4x8 slice. The times are simulated.
256 devices in a mesh: seq: 32 (over z, x), head: 8 (over y, core).
Axes of the slice: x: 4, y: 4, z: 8, core: 2. Of those that a mesh axis runs over, the one named last changes fastest.
Arguments:
- queries: bfloat16 [8192, 1024], P('seq', 'head'), may hold values from -16 to 16
- keys: bfloat16 [8192, 1024], P(('seq', 'head')), may hold values from -16 to 16
- values: bfloat16 [8192, 1024], P(('seq', 'head')), may hold values from -6 to 6
- out_grad: bfloat16 [8192, 1024], P('seq', 'head'), may hold values from -6 to 6
Outputs:
- attended: bfloat16 [8192, 1024], P('seq', 'head')
- query_grad: float32 [8192, 1024], P('seq', 'head')
- key_grad: float32 [8192, 1024], P('seq', 'head')
- value_grad: float32 [8192, 1024], P('seq', 'head')
All inputs are finite; a program needn't handle non-finite values.
Results may differ from a plain program's by a relative error of at most 0.0095.
Values may be sent and summed in bfloat16 or wider, within the bound.
No kernel may reach another device: no remote copies, remote signals or barrier semaphores. Data moves between devices by JAX's collectives and lax.ppermute only.
A program may use at most 64 MiB of HBM per device.

v0:
```python
import math
import jax
import jax.numpy as jnp
from jax import lax
from jax.sharding import Mesh
from jax.sharding import PartitionSpec as P

SEQ = ("seq_0", "seq_1")
SEQ_HEAD = ("seq_0", "seq_1", "head")
masked_value = -1e30


def whole_of(array, axes, dim):
    filled = array
    for number in range(len(axes) - 1, -1, -1):
        filled = lax.all_gather(filled, axes[number], axis=dim, tiled=True)
    return filled


def joined_along(parts, dim):
    dims = list(parts.shape[1:])
    dims[dim] *= parts.shape[0]
    return jnp.moveaxis(parts, 0, dim).reshape(dims)


def gather_packed(arrays, axis, dims):
    ravelled = jnp.concatenate([a.reshape(-1) for a in arrays])
    lines, at, gathered = (lax.all_gather(ravelled, axis), 0, [])
    for a, dim in zip(arrays, dims):
        parts = lines[:, at : at + a.size].reshape(-1, *a.shape)
        gathered.append(joined_along(parts, dim))
        at += a.size
    return tuple(gathered)


def key_block(length, row_count):
    return min(length, max(1024, 2 * row_count))


def attend_range(queries, qstart, whole_keys, whole_values, key_low, key_high, scaling):
    row_count, head_width = queries.shape
    length = whole_keys.shape[0]
    span_rows = key_block(length, row_count)
    query_pos = qstart + jnp.arange(row_count, dtype=jnp.int32)

    def attend_compute(running, kstart):
        weighted, rowmax, rowsum = running
        key_piece = lax.dynamic_slice_in_dim(whole_keys, kstart, span_rows, 0)
        value_piece = lax.dynamic_slice_in_dim(whole_values, kstart, span_rows, 0)
        key_pos = kstart + jnp.arange(span_rows, dtype=jnp.int32)
        allowed = (
            (key_pos[None, :] <= query_pos[:, None])
            & (key_pos[None, :] >= key_low)
            & (key_pos[None, :] < key_high)
        )
        scores = (
            jnp.einsum("qd,kd->qk", queries, key_piece, preferred_element_type=jnp.float32)
            * scaling
        )
        scores = jnp.where(allowed, scores, masked_value)
        new_max = jnp.maximum(rowmax, jnp.max(scores, axis=1))
        weights = jnp.where(allowed, jnp.exp(scores - new_max[:, None]), 0.0)
        factor = jnp.exp(rowmax - new_max)
        rowsum = rowsum * factor + jnp.sum(weights, axis=1)
        weighted = weighted * factor[:, None] + jnp.dot(
            weights.astype(jnp.bfloat16), value_piece, preferred_element_type=jnp.float32
        )
        return (weighted, new_max, rowsum)

    def attend_advance(counter, running):
        kstart = counter * span_rows
        needed = (
            (kstart < key_high) & (kstart + span_rows > key_low) & (kstart < qstart + row_count)
        )
        return lax.cond(
            needed,
            lambda previous: attend_compute(previous, kstart),
            lambda previous: previous,
            running,
        )

    initial = (
        jnp.zeros((row_count, head_width), jnp.float32),
        jnp.full((row_count,), masked_value, jnp.float32),
        jnp.zeros((row_count,), jnp.float32),
    )
    return lax.fori_loop(0, length // span_rows, attend_advance, initial)


def backward_range(
    queries,
    out_grad,
    log_norm,
    row_delta,
    qstart,
    whole_keys,
    whole_values,
    key_low,
    key_high,
    scaling,
):
    row_count, head_width = queries.shape
    length = whole_keys.shape[0]
    span_rows = key_block(length, row_count)
    query_pos = qstart + jnp.arange(row_count, dtype=jnp.int32)

    def backward_compute(running, kstart):
        query_part, terms = running
        key_piece = lax.dynamic_slice_in_dim(whole_keys, kstart, span_rows, 0)
        value_piece = lax.dynamic_slice_in_dim(whole_values, kstart, span_rows, 0)
        key_pos = kstart + jnp.arange(span_rows, dtype=jnp.int32)
        allowed = (
            (key_pos[None, :] <= query_pos[:, None])
            & (key_pos[None, :] >= key_low)
            & (key_pos[None, :] < key_high)
        )
        scores = (
            jnp.einsum("qd,kd->qk", queries, key_piece, preferred_element_type=jnp.float32)
            * scaling
        )
        probs = jnp.where(allowed, jnp.exp(scores - log_norm[:, None]), 0.0)
        grad_probs = jnp.einsum(
            "qd,kd->qk", out_grad, value_piece, preferred_element_type=jnp.float32
        )
        grad_scores = (probs * (grad_probs - row_delta[:, None]) * scaling).astype(jnp.bfloat16)
        query_part = query_part + jnp.dot(
            grad_scores, key_piece, preferred_element_type=jnp.float32
        )
        return (query_part, terms)

    def backward_advance(counter, running):
        kstart = counter * span_rows
        needed = (
            (kstart < key_high) & (kstart + span_rows > key_low) & (kstart < qstart + row_count)
        )
        return lax.cond(
            needed,
            lambda previous: backward_compute(previous, kstart),
            lambda previous: previous,
            running,
        )

    initial = (jnp.zeros((row_count, head_width), jnp.float32), None)
    return lax.fori_loop(0, length // span_rows, backward_advance, initial)


def key_range(all_rows, all_grads, all_norms, all_deltas, own_keys, own_values, kstart, scaling):
    length = all_rows.shape[0]
    row_count, head_width = own_keys.shape
    span_rows = key_block(length, row_count)
    key_pos = kstart + jnp.arange(row_count, dtype=jnp.int32)

    def key_compute(running, qstart):
        key_total, value_total = running
        query_piece = lax.dynamic_slice_in_dim(all_rows, qstart, span_rows, 0)
        grad_piece = lax.dynamic_slice_in_dim(all_grads, qstart, span_rows, 0)
        norm_piece = lax.dynamic_slice_in_dim(all_norms, qstart, span_rows, 0)
        delta_piece = lax.dynamic_slice_in_dim(all_deltas, qstart, span_rows, 0)
        query_pos = qstart + jnp.arange(span_rows, dtype=jnp.int32)
        allowed = key_pos[None, :] <= query_pos[:, None]
        scores = (
            jnp.einsum("qd,kd->qk", query_piece, own_keys, preferred_element_type=jnp.float32)
            * scaling
        )
        probs = jnp.where(allowed, jnp.exp(scores - norm_piece[:, None]), 0.0)
        grad_probs = jnp.einsum(
            "qd,kd->qk", grad_piece, own_values, preferred_element_type=jnp.float32
        )
        grad_scores = (probs * (grad_probs - delta_piece[:, None]) * scaling).astype(jnp.bfloat16)
        key_total = key_total + jnp.einsum(
            "qk,qd->kd", grad_scores, query_piece, preferred_element_type=jnp.float32
        )
        value_total = value_total + jnp.einsum(
            "qk,qd->kd", probs.astype(jnp.bfloat16), grad_piece, preferred_element_type=jnp.float32
        )
        return (key_total, value_total)

    def key_advance(counter, running):
        qstart = counter * span_rows
        needed = qstart + span_rows > kstart
        return lax.cond(
            needed,
            lambda previous: key_compute(previous, qstart),
            lambda previous: previous,
            running,
        )

    initial = (
        jnp.zeros((row_count, head_width), jnp.float32),
        jnp.zeros((row_count, head_width), jnp.float32),
    )
    return lax.fori_loop(0, length // span_rows, key_advance, initial)


def per_device(queries, keys, values, out_grad):
    row_count, head_width = queries.shape
    scaling = 1.0 / math.sqrt(head_width)
    local_keys, local_values = (
        lax.all_to_all(keys, "head", split_axis=1, concat_axis=0, tiled=True),
        lax.all_to_all(values, "head", split_axis=1, concat_axis=0, tiled=True),
    )
    whole_keys, whole_values = (whole_of(local_keys, SEQ, 0), whole_of(local_values, SEQ, 0))
    length = whole_keys.shape[0]
    device = lax.axis_index(SEQ)
    qstart = device * row_count
    weighted, rowmax, rowsum = attend_range(
        queries, qstart, whole_keys, whole_values, 0, length, scaling
    )
    output = weighted / rowsum[:, None]
    log_norm = rowmax + jnp.log(rowsum)
    attended = output.astype(jnp.bfloat16)
    row_delta = jnp.sum(out_grad.astype(jnp.float32) * output, axis=1)
    query_grad, unused = backward_range(
        queries, out_grad, log_norm, row_delta, qstart, whole_keys, whole_values, 0, length, scaling
    )
    all_rows, all_grads = (whole_of(queries, SEQ, 0), whole_of(out_grad, SEQ, 0))
    all_norms, all_deltas = gather_packed((log_norm, row_delta), SEQ, (0, 0))
    key_grad, value_grad = key_range(
        all_rows, all_grads, all_norms, all_deltas, local_keys, local_values, qstart, scaling
    )
    return (attended, query_grad, key_grad, value_grad)


def solution(mesh):
    split = Mesh(mesh.devices.reshape(8, 4, mesh.shape["head"]), ("seq_0", "seq_1", "head"))
    return jax.shard_map(
        per_device,
        mesh=split,
        in_specs=(P(SEQ, "head"), P(SEQ_HEAD, None), P(SEQ_HEAD, None), P(SEQ, "head")),
        out_specs=(P(SEQ, "head"), P(SEQ, "head"), P(SEQ, "head"), P(SEQ, "head")),
        check_vma=False,
    )
```

profile of v0, /device:TPU:8, one launch (start us, length us, event | category | flops | bytes accessed | tf_op | source)
XLA Modules:
  0.0 247.4 jit_solution(4875026922688107261)
XLA Ops:
  7.2 0.0 all-gather.7.cloned.1.call-start
  7.2 0.8 copy-done
  8.0 8.9 %all_to_all.38 = bf16[32,8,128]{2,0,1:T(8,128)(2,1)S(1)} all-to-all(bf16[32,8,128]{2,0,1:T(8,128)(2,1)S(1)} %copy_bitcast_fusion.1), channel_id=1, replica_groups=mesh['seq_0'=8,'seq_1'=4,'head'=8] {'head'}, dimensions={1} | all-to-all | bytes 131072 | tf_op jit(solution)/shard_map/all_to_all | solution.py:199
  16.9 13.3 %all_gather.30 = bf16[1024,128]{1,0:T(8,128)(2,1)} all-gather(bf16[256,128]{1,0:T(8,128)(2,1)S(1)} %bitcast.53), channel_id=1, replica_groups=mesh['seq_0'=8,'seq_1'=4,'head'=8] {'seq_1'}, dimensions={0}, use_global_device_ids=true | all-gather | bytes 327680 | tf_op jit(solution)/shard_map/all_gather | solution.py:16
  30.3 0.0 all-gather.9.cloned.1.call-start
  30.3 0.9 copy_bitcast_fusion
  31.2 8.0 %all_to_all.39 = bf16[32,8,128]{2,0,1:T(8,128)(2,1)S(1)} all-to-all(bf16[32,8,128]{2,0,1:T(8,128)(2,1)S(1)} %copy_bitcast_fusion), channel_id=1, replica_groups=mesh['seq_0'=8,'seq_1'=4,'head'=8] {'head'}, dimensions={1} | all-to-all | bytes 131072 | tf_op jit(solution)/shard_map/all_to_all | solution.py:200
  39.2 13.0 %all_gather.32 = bf16[1024,128]{1,0:T(8,128)(2,1)} all-gather(bf16[256,128]{1,0:T(8,128)(2,1)S(1)} %bitcast.51), channel_id=1, replica_groups=mesh['seq_0'=8,'seq_1'=4,'head'=8] {'seq_1'}, dimensions={0}, use_global_device_ids=true | all-gather | bytes 327680 | tf_op jit(solution)/shard_map/all_gather | solution.py:16
  52.2 0.0 all-gather.9.cloned.1.call-update
  52.2 0.0 all-gather.11.cloned.1.call-start
  52.2 14.0 %all_gather.34 = bf16[1024,128]{1,0:T(8,128)(2,1)} all-gather(bf16[256,128]{1,0:T(8,128)(2,1)} %param.16), channel_id=1, replica_groups=mesh['seq_0'=8,'seq_1'=4,'head'=8] {'seq_1'}, dimensions={0}, use_global_device_ids=true | all-gather | bytes 327680 | tf_op jit(solution)/shard_map/all_gather | solution.py:16
  66.3 0.0 all-gather.13.cloned.1.call-start
  66.4 13.1 %all_gather.38 = bf16[1024,128]{1,0:T(8,128)(2,1)} all-gather(bf16[256,128]{1,0:T(8,128)(2,1)S(1)} %copy-done.4), channel_id=1, replica_groups=mesh['seq_0'=8,'seq_1'=4,'head'=8] {'seq_1'}, dimensions={0}, use_global_device_ids=true | all-gather | bytes 327680 | tf_op jit(solution)/shard_map/all_gather | solution.py:16
  79.5 0.0 all-gather.13.cloned.1.call-update
  79.5 0.0 all-gather.7.cloned.1.call-done
  79.5 34.4 %all-gather.9.cloned.1.call-done = bf16[8192,128]{1,0:T(8,128)(2,1)} async-done(((bf16[1024,128]{1,0:T(8,128)(2,1)}), bf16[8192,128]{1,0:T(8,128)(2,1)}) %all-gather.9.cloned.1.call-update) | async-done | bytes 2097168 | tf_op jit(solution)/shard_map/all_gather | solution.py:16
  113.9 5.1 %while.56 = (s32[]{:T(128)}, f32[256,128]{1,0:T(8,128)S(1)}, f32[256]{0:T(256)S(1)}, f32[256]{0:T(256)S(1)}, s32[]{:T(128)}, /*index=5*/bf16[8192,128]{1,0:T(8,1...) while((s32[]{:T(128)}, f32[256,128]{1,0:T(8,128)S(1)}, ...), condition=%wide.region_5.6_spmd.clone, body=%wide.region_0.5_spmd.clone.sunk | while | flops 139006736 | bytes 4045177 | solution.py:87
  114.0 4.6 %conditional.10 = ((f32[256,128]{1,0:T(8,128)S(1)}, f32[256]{0:T(256)S(1)}, f32[256]{0:T(256)S(1)})) conditional(s32[]{:T(128)} %convert_element_type.68, (f32[256,128]{1,0:T(8,128)S(1)}, f32[256]{0:T(256)S(1)}, f32[256]{0:T(256)S(1)}) %tuple.146, (s32[]{:T(128)}, s32[]{:T(128)}, bf16[8192,128]{1,0:T(8,128)(2,1)}, bf16[256,128]{1,0:T(8,128)(2,1)S(1)}, ...), branch_computations={%region_1.0_spmd, %region_2.4_spmd} | conditional | flops 139006720 | bytes 4043862 | solution.py:75
  114.1 1.9 fusion.68
  115.9 0.8 fusion.8
  116.8 1.8 convolution_add_fusion
  119.1 0.7 multiply_reduce_fusion
  119.8 80.2 %all-gather.1 = f32[32,1,512]{2,1,0:T(1,128)S(1)} all-gather(f32[1,1,512]{2,1,0:T(1,128)S(1)} %bitcast.58), channel_id=2, replica_groups=mesh['seq_0'=8,'seq_1'=4,'head'=8] {'seq_0','seq_1'}, dimensions={0}, use_global_device_ids=true | all-gather | bytes 67584 | tf_op jit(solution)/shard_map/all_gather | solution.py:28
  200.1 3.5 %while.57 = (s32[]{:T(128)}, f32[256,128]{1,0:T(8,128)S(1)}, s32[]{:T(128)}, bf16[8192,128]{1,0:T(8,128)(2,1)}, bf16[256,128]{1,0:T(8,128)(2,1)S(1)}, /*index=5*...) while((s32[]{:T(128)}, f32[256,128]{1,0:T(8,128)S(1)}, ...), condition=%wide.region_10.11_spmd.clone, body=%wide.region_7.10_spmd.clone.sunk | while | flops 203985168 | bytes 3296597 | solution.py:144
  200.2 3.0 %conditional.11 = (f32[256,128]{1,0:T(8,128)S(1)}) conditional(s32[]{:T(128)} %convert_element_type.69, f32[256,128]{1,0:T(8,128)S(1)} %get-tuple-element.1194, (s32[]{:T(128)}, s32[]{:T(128)}, bf16[8192,128]{1,0:T(8,128)(2,1)}, bf16[256,128]{1,0:T(8,128)(2,1)S(1)}, f32[256]{0:T(256)S(1)}, /*index=5*/bf16[8192,128]{1,0:T(8,128)(2,1)}, ...), branch_computations={%region_8.8_spmd, %region_9.9_spmd} | conditional | flops 203985152 | bytes 3295290 | solution.py:136
  200.2 1.4 fusion.30
  201.7 1.5 fusion.33
  203.6 0.0 all-gather.11.cloned.1.call-done
  203.7 0.6 copy-done.3
  204.3 35.9 %while.58 = (s32[]{:T(128)}, f32[256,128]{1,0:T(8,128)S(1)}, f32[256,128]{1,0:T(8,128)S(1)}, s32[]{:T(128)}, bf16[8192,128]{1,0:T(8,128)(2,1)}, /*index=5*/bf16[...) while((s32[]{:T(128)}, f32[256,128]{1,0:T(8,128)S(1)}, ...), condition=%wide.region_14.15_spmd.clone.clone, body=%wide.region_11.14_spmd.clone.clone.sunk | while | flops 270861568 | bytes 4887901 | solution.py:192
  204.3 4.4 %conditional.12 = ((f32[256,128]{1,0:T(8,128)S(1)}, f32[256,128]{1,0:T(8,128)S(1)})) conditional(s32[]{:T(128)} %convert_element_type.70, (f32[256,128]{1,0:T(8,128)S(1)}, f32[256,128]{1,0:T(8,128)S(1)}) %tuple.151, (s32[]{:T(128)}, s32[]{:T(128)}, bf16[8192,128]{1,0:T(8,128)(2,1)}, bf16[256,128]{1,0:T(8,128)(2,1)S(1)}, f32[8192]{0:T(1024)S(1)}, ...), branch_computations={%region_12.12_spmd, %region_13.13_spmd} | conditional | flops 270861568 | bytes 4886610 | solution.py:181
  204.3 1.4 fusion.50
  205.7 1.7 fusion.53
  207.4 1.3 convolution_add_fusion.1
  208.7 4.5 %conditional.12 = ((f32[256,128]{1,0:T(8,128)S(1)}, f32[256,128]{1,0:T(8,128)S(1)})) conditional(s32[]{:T(128)} %convert_element_type.70, (f32[256,128]{1,0:T(8,128)S(1)}, f32[256,128]{1,0:T(8,128)S(1)}) %tuple.151, (s32[]{:T(128)}, s32[]{:T(128)}, bf16[8192,128]{1,0:T(8,128)(2,1)}, bf16[256,128]{1,0:T(8,128)(2,1)S(1)}, f32[8192]{0:T(1024)S(1)}, ...), branch_computations={%region_12.12_spmd, %region_13.13_spmd} | conditional | flops 270861568 | bytes 4886610 | solution.py:181
  208.8 1.4 fusion.50
  210.2 1.7 fusion.53
  211.9 1.3 convolution_add_fusion.1
  213.2 4.5 %conditional.12 = ((f32[256,128]{1,0:T(8,128)S(1)}, f32[256,128]{1,0:T(8,128)S(1)})) conditional(s32[]{:T(128)} %convert_element_type.70, (f32[256,128]{1,0:T(8,128)S(1)}, f32[256,128]{1,0:T(8,128)S(1)}) %tuple.151, (s32[]{:T(128)}, s32[]{:T(128)}, bf16[8192,128]{1,0:T(8,128)(2,1)}, bf16[256,128]{1,0:T(8,128)(2,1)S(1)}, f32[8192]{0:T(1024)S(1)}, ...), branch_computations={%region_12.12_spmd, %region_13.13_spmd} | conditional | flops 270861568 | bytes 4886610 | solution.py:181
  213.3 1.4 fusion.50
  214.7 1.7 fusion.53
  216.4 1.3 convolution_add_fusion.1
  217.7 4.5 %conditional.12 = ((f32[256,128]{1,0:T(8,128)S(1)}, f32[256,128]{1,0:T(8,128)S(1)})) conditional(s32[]{:T(128)} %convert_element_type.70, (f32[256,128]{1,0:T(8,128)S(1)}, f32[256,128]{1,0:T(8,128)S(1)}) %tuple.151, (s32[]{:T(128)}, s32[]{:T(128)}, bf16[8192,128]{1,0:T(8,128)(2,1)}, bf16[256,128]{1,0:T(8,128)(2,1)S(1)}, f32[8192]{0:T(1024)S(1)}, ...), branch_computations={%region_12.12_spmd, %region_13.13_spmd} | conditional | flops 270861568 | bytes 4886610 | solution.py:181
  217.8 1.4 fusion.50
  219.2 1.7 fusion.53
  220.9 1.3 convolution_add_fusion.1
  222.2 4.5 %conditional.12 = ((f32[256,128]{1,0:T(8,128)S(1)}, f32[256,128]{1,0:T(8,128)S(1)})) conditional(s32[]{:T(128)} %convert_element_type.70, (f32[256,128]{1,0:T(8,128)S(1)}, f32[256,128]{1,0:T(8,128)S(1)}) %tuple.151, (s32[]{:T(128)}, s32[]{:T(128)}, bf16[8192,128]{1,0:T(8,128)(2,1)}, bf16[256,128]{1,0:T(8,128)(2,1)S(1)}, f32[8192]{0:T(1024)S(1)}, ...), branch_computations={%region_12.12_spmd, %region_13.13_spmd} | conditional | flops 270861568 | bytes 4886610 | solution.py:181
  222.3 1.4 fusion.50
  223.7 1.7 fusion.53
  225.4 1.3 convolution_add_fusion.1
  226.7 4.5 %conditional.12 = ((f32[256,128]{1,0:T(8,128)S(1)}, f32[256,128]{1,0:T(8,128)S(1)})) conditional(s32[]{:T(128)} %convert_element_type.70, (f32[256,128]{1,0:T(8,128)S(1)}, f32[256,128]{1,0:T(8,128)S(1)}) %tuple.151, (s32[]{:T(128)}, s32[]{:T(128)}, bf16[8192,128]{1,0:T(8,128)(2,1)}, bf16[256,128]{1,0:T(8,128)(2,1)S(1)}, f32[8192]{0:T(1024)S(1)}, ...), branch_computations={%region_12.12_spmd, %region_13.13_spmd} | conditional | flops 270861568 | bytes 4886610 | solution.py:181
  226.8 1.4 fusion.50
  228.2 1.7 fusion.53
  229.9 1.3 convolution_add_fusion.1
  231.2 4.5 %conditional.12 = ((f32[256,128]{1,0:T(8,128)S(1)}, f32[256,128]{1,0:T(8,128)S(1)})) conditional(s32[]{:T(128)} %convert_element_type.70, (f32[256,128]{1,0:T(8,128)S(1)}, f32[256,128]{1,0:T(8,128)S(1)}) %tuple.151, (s32[]{:T(128)}, s32[]{:T(128)}, bf16[8192,128]{1,0:T(8,128)(2,1)}, bf16[256,128]{1,0:T(8,128)(2,1)S(1)}, f32[8192]{0:T(1024)S(1)}, ...), branch_computations={%region_12.12_spmd, %region_13.13_spmd} | conditional | flops 270861568 | bytes 4886610 | solution.py:181
  231.3 1.4 fusion.50
  232.7 1.7 fusion.53
  234.4 1.3 convolution_add_fusion.1
  235.7 4.5 %conditional.12 = ((f32[256,128]{1,0:T(8,128)S(1)}, f32[256,128]{1,0:T(8,128)S(1)})) conditional(s32[]{:T(128)} %convert_element_type.70, (f32[256,128]{1,0:T(8,128)S(1)}, f32[256,128]{1,0:T(8,128)S(1)}) %tuple.151, (s32[]{:T(128)}, s32[]{:T(128)}, bf16[8192,128]{1,0:T(8,128)(2,1)}, bf16[256,128]{1,0:T(8,128)(2,1)S(1)}, f32[8192]{0:T(1024)S(1)}, ...), branch_computations={%region_12.12_spmd, %region_13.13_spmd} | conditional | flops 270861568 | bytes 4886610 | solution.py:181
  235.8 1.4 fusion.50
  237.2 1.7 fusion.53
  238.9 1.3 convolution_add_fusion.1
  240.2 0.6 copy-done.1
  240.8 0.0 copy-done.2
  (103 shorter events, 0.8 us)
Async XLA Ops:
  7.2 0.8 copy-start
  7.2 106.8 %copy-start.5 = (bf16[256,128]{1,0:T(8,128)(2,1)S(1)}, bf16[256,128]{1,0:T(8,128)(2,1)}, u32[]{:S(2)}) copy-start(bf16[256,128]{1,0:T(8,128)(2,1)} %param.16) | copy-start | bytes 196612
  7.2 59.2 %copy-start.4 = (bf16[256,128]{1,0:T(8,128)(2,1)S(1)}, bf16[256,128]{1,0:T(8,128)(2,1)}, u32[]{:S(2)}) copy-start(bf16[256,128]{1,0:T(8,128)(2,1)} %param.19) | copy-start | bytes 196612
  7.2 72.3 %all-gather.7.cloned.1.call-start = ((), (), s32[]{:S(2)}) async-start(), calls=%async_computation.2 | async-start | bytes 2359296 | tf_op jit(solution)/shard_map/all_gather | solution.py:16
  30.3 83.6 %all-gather.9.cloned.1.call-start = ((), (), s32[]{:S(2)}) async-start(), calls=%async_computation.3 | async-start | bytes 2359296 | tf_op jit(solution)/shard_map/all_gather | solution.py:16
  52.2 151.4 %all-gather.11.cloned.1.call-start = ((), (), s32[]{:S(2)}) async-start(), calls=%async_computation.4 | async-start | bytes 2359296 | tf_op jit(solution)/shard_map/all_gather | solution.py:16
  66.3 137.4 %all-gather.13.cloned.1.call-start = ((), (), s32[]{:S(2)}) async-start(), calls=%async_computation.5 | async-start | bytes 2359296 | tf_op jit(solution)/shard_map/all_gather | solution.py:16
  203.6 0.7 copy-start.3
  240.2 0.7 copy-start.1
  240.2 0.7 copy-start.2
Sparse Core Ops, SparseCore 0:
  30.4 42.2 all-gather.6
  74.5 39.4 all-gather.8
  115.7 39.4 all-gather.10
  156.8 39.5 all-gather.12
where the time goes:
time: 249 us; the launch traced here: 247 us
  blocking collectives  151 us (61%)
  matrix products  41.4 us (17%)
  waiting for transfers between devices  34.5 us (14%)
  between operations  14 us (6%)
  local copies, waits for them, and re-layouts  3.2 us (1%)
    all_gather x1, blocking collectives, gather_packed(): lines, at, gathered = (lax.all_gather(ravelled, axis), 0, [])  80.2 us
    all_gather x4, blocking collectives, whole_of(): filled = lax.all_gather(filled, axes[number], axis=dim, tiled=True)  53.5 us
    all_gather x4, waiting for transfers between devices, whole_of(): filled = lax.all_gather(filled, axes[number], axis=dim, tiled=True)  34.4 us
    dot_general x8, matrix products, key_compute(): jnp.einsum('qk,qd->kd', grad_scores, query_piece, preferred_element_type=...  13.6 us
    dot_general x8, matrix products, key_compute(): jnp.einsum('qd,kd->qk', query_piece, own_keys, preferred_element_type=jnp...  10.8 us
    dot_general x8, matrix products, key_compute(): jnp.einsum('qk,qd->kd', probs.astype(jnp.bfloat16), grad_piece, preferred...  10.4 us
    all_to_all x1, blocking collectives, per_device(): lax.all_to_all(keys, 'head', split_axis=1, concat_axis=0, tiled=True)  8.88 us
    all_to_all x1, blocking collectives, per_device(): lax.all_to_all(values, 'head', split_axis=1, concat_axis=0, tiled=True)  8 us
  transfers between devices with their start and end apart: 4, of which 1 were waited for; matrix products, arithmetic and copies ran while one was open for 4% of the time, Pallas kernels for 0%

commit v1 on v0

--- a/solution.py
+++ b/solution.py
@@ -196,7 +196,15 @@
     row_count, head_width = queries.shape
     scaling = 1.0 / math.sqrt(head_width)
     local_keys, local_values = (
-        lax.all_to_all(keys, "head", split_axis=1, concat_axis=0, tiled=True),
+        jnp.concatenate(
+            lax.all_to_all(
+                jnp.stack(jnp.split(keys, lax.axis_size("head"), 1), 0),
+                concat_axis=0,
+                axis_name="head",
+                split_axis=0,
+            ),
+            0,
+        ),
         lax.all_to_all(values, "head", split_axis=1, concat_axis=0, tiled=True),
     )
     whole_keys, whole_values = (whole_of(local_keys, SEQ, 0), whole_of(local_values, SEQ, 0))

time: 249 us -> 254 us (1.020)
  local copies, waits for them, and re-layouts: 3.2 us -> 7.29 us
    unnamed x16 -> x23, local copies, waits for them, and re-layouts: 2.07 us -> 6.3 us
  transfers between devices with their start and end apart: 4 -> 4, of which waited for: 1 -> 1; matrix products, arithmetic and copies ran while one was open for 4% -> 3% of each run, Pallas kernels for 0% -> 0%
where the time goes in v1:
time: 254 us; the launch traced here: 252 us
  blocking collectives  151 us (59%)
  matrix products  41.5 us (16%)
  waiting for transfers between devices  34.9 us (14%)
  between operations  14 us (6%)
  local copies, waits for them, and re-layouts  7.29 us (3%)
    all_gather x1, blocking collectives, gather_packed(): lines, at, gathered = (lax.all_gather(ravelled, axis), 0, [])  80.2 us
    all_gather x4, blocking collectives, whole_of(): filled = lax.all_gather(filled, axes[number], axis=dim, tiled=True)  53.9 us
    all_gather x4, waiting for transfers between devices, whole_of(): filled = lax.all_gather(filled, axes[number], axis=dim, tiled=True)  34.8 us
    dot_general x8, matrix products, key_compute(): jnp.einsum('qk,qd->kd', grad_scores, query_piece, preferred_element_type=...  13.6 us
    dot_general x8, matrix products, key_compute(): jnp.einsum('qd,kd->qk', query_piece, own_keys, preferred_element_type=jnp...  10.9 us
    dot_general x8, matrix products, key_compute(): jnp.einsum('qk,qd->kd', probs.astype(jnp.bfloat16), grad_piece, preferred...  10.4 us
    all_to_all x1, blocking collectives, per_device(): lax.all_to_all(jnp.stack(jnp.split(keys, lax.axis_size('head'), 1), 0), c...  8.87 us
    all_to_all x1, blocking collectives, per_device(): lax.all_to_all(values, 'head', split_axis=1, concat_axis=0, tiled=True)  8 us
  transfers between devices with their start and end apart: 4, of which 1 were waited for; matrix products, arithmetic and copies ran while one was open for 3% of the time, Pallas kernels for 0%

profile of v1, /device:TPU:8, one launch (start us, length us, event | category | flops | bytes accessed | tf_op | source)
XLA Modules:
  0.0 252.4 jit_solution(7943227475381176916)
XLA Ops:
  7.2 0.7 constant_dynamic-update-slice_fusion.7
  8.0 0.7 constant_dynamic-update-slice_fusion.6
  8.7 0.7 constant_dynamic-update-slice_fusion.5
  9.4 0.7 constant_dynamic-update-slice_fusion.4
  10.1 0.7 constant_dynamic-update-slice_fusion.3
  10.8 0.7 constant_dynamic-update-slice_fusion.2
  11.5 0.7 constant_dynamic-update-slice_fusion.1
  12.2 0.7 constant_dynamic-update-slice_fusion
  13.0 8.9 %all_to_all.24 = bf16[8,32,128]{2,1,0:T(8,128)(2,1)S(1)} all-to-all(bf16[8,32,128]{2,1,0:T(8,128)(2,1)S(1)} %constant_dynamic-update-slice_fusion), channel_id=1, replica_groups=mesh['seq_0'=8,'seq_1'=4,'head'=8] {'head'}, dimensions={0} | all-to-all | bytes 131072 | tf_op jit(solution)/shard_map/all_to_all | solution.py:200
  21.8 13.3 %all_gather.30 = bf16[1024,128]{1,0:T(8,128)(2,1)} all-gather(bf16[256,128]{1,0:T(8,128)(2,1)S(1)} %bitcast.62), channel_id=1, replica_groups=mesh['seq_0'=8,'seq_1'=4,'head'=8] {'seq_1'}, dimensions={0}, use_global_device_ids=true | all-gather | bytes 327680 | tf_op jit(solution)/shard_map/all_gather | solution.py:16
  35.2 0.0 all-gather.9.cloned.1.call-start
  35.3 8.0 %all_to_all.25 = bf16[32,8,128]{2,0,1:T(8,128)(2,1)S(1)} all-to-all(bf16[32,8,128]{2,0,1:T(8,128)(2,1)S(1)} %copy_bitcast_fusion), channel_id=1, replica_groups=mesh['seq_0'=8,'seq_1'=4,'head'=8] {'head'}, dimensions={1} | all-to-all | bytes 131072 | tf_op jit(solution)/shard_map/all_to_all | solution.py:208
  43.3 13.0 %all_gather.32 = bf16[1024,128]{1,0:T(8,128)(2,1)} all-gather(bf16[256,128]{1,0:T(8,128)(2,1)S(1)} %bitcast.60), channel_id=1, replica_groups=mesh['seq_0'=8,'seq_1'=4,'head'=8] {'seq_1'}, dimensions={0}, use_global_device_ids=true | all-gather | bytes 327680 | tf_op jit(solution)/shard_map/all_gather | solution.py:16
  56.3 0.0 all-gather.11.cloned.1.call-start
  56.3 14.3 %all_gather.34 = bf16[1024,128]{1,0:T(8,128)(2,1)} all-gather(bf16[256,128]{1,0:T(8,128)(2,1)} %param.16), channel_id=1, replica_groups=mesh['seq_0'=8,'seq_1'=4,'head'=8] {'seq_1'}, dimensions={0}, use_global_device_ids=true | all-gather | bytes 327680 | tf_op jit(solution)/shard_map/all_gather | solution.py:16
  70.7 13.3 %all_gather.38 = bf16[1024,128]{1,0:T(8,128)(2,1)} all-gather(bf16[256,128]{1,0:T(8,128)(2,1)S(1)} %copy-done.4), channel_id=1, replica_groups=mesh['seq_0'=8,'seq_1'=4,'head'=8] {'seq_1'}, dimensions={0}, use_global_device_ids=true | all-gather | bytes 327680 | tf_op jit(solution)/shard_map/all_gather | solution.py:16
  84.0 34.8 %all-gather.9.cloned.1.call-done = bf16[8192,128]{1,0:T(8,128)(2,1)} async-done(((bf16[1024,128]{1,0:T(8,128)(2,1)}), bf16[8192,128]{1,0:T(8,128)(2,1)}) %all-gather.9.cloned.1.call-update) | async-done | bytes 2097168 | tf_op jit(solution)/shard_map/all_gather | solution.py:16
  118.9 5.1 %while.56 = (s32[]{:T(128)}, f32[256,128]{1,0:T(8,128)S(1)}, f32[256]{0:T(256)S(1)}, f32[256]{0:T(256)S(1)}, s32[]{:T(128)}, /*index=5*/bf16[8192,128]{1,0:T(8,1...) while((s32[]{:T(128)}, f32[256,128]{1,0:T(8,128)S(1)}, ...), condition=%wide.region_5.6_spmd.clone, body=%wide.region_0.5_spmd.clone.sunk | while | flops 139006736 | bytes 4045177 | solution.py:87
  118.9 4.6 %conditional.10 = ((f32[256,128]{1,0:T(8,128)S(1)}, f32[256]{0:T(256)S(1)}, f32[256]{0:T(256)S(1)})) conditional(s32[]{:T(128)} %convert_element_type.68, (f32[256,128]{1,0:T(8,128)S(1)}, f32[256]{0:T(256)S(1)}, f32[256]{0:T(256)S(1)}) %tuple.146, (s32[]{:T(128)}, s32[]{:T(128)}, bf16[8192,128]{1,0:T(8,128)(2,1)}, bf16[256,128]{1,0:T(8,128)(2,1)S(1)}, ...), branch_computations={%region_1.0_spmd, %region_2.4_spmd} | conditional | flops 139006720 | bytes 4043862 | solution.py:75
  119.0 1.9 fusion.68
  120.8 0.8 fusion.8
  121.7 1.8 convolution_add_fusion
  124.0 0.7 multiply_reduce_fusion
  124.8 80.2 %all-gather.1 = f32[32,1,512]{2,1,0:T(1,128)S(1)} all-gather(f32[1,1,512]{2,1,0:T(1,128)S(1)} %bitcast.67), channel_id=2, replica_groups=mesh['seq_0'=8,'seq_1'=4,'head'=8] {'seq_0','seq_1'}, dimensions={0}, use_global_device_ids=true | all-gather | bytes 67584 | tf_op jit(solution)/shard_map/all_gather | solution.py:28
  205.0 3.5 %while.57 = (s32[]{:T(128)}, f32[256,128]{1,0:T(8,128)S(1)}, s32[]{:T(128)}, bf16[8192,128]{1,0:T(8,128)(2,1)}, bf16[256,128]{1,0:T(8,128)(2,1)S(1)}, /*index=5*...) while((s32[]{:T(128)}, f32[256,128]{1,0:T(8,128)S(1)}, ...), condition=%wide.region_10.11_spmd.clone, body=%wide.region_7.10_spmd.clone.sunk | while | flops 203985168 | bytes 3296597 | solution.py:144
  205.1 3.0 %conditional.11 = (f32[256,128]{1,0:T(8,128)S(1)}) conditional(s32[]{:T(128)} %convert_element_type.69, f32[256,128]{1,0:T(8,128)S(1)} %get-tuple-element.1194, (s32[]{:T(128)}, s32[]{:T(128)}, bf16[8192,128]{1,0:T(8,128)(2,1)}, bf16[256,128]{1,0:T(8,128)(2,1)S(1)}, f32[256]{0:T(256)S(1)}, /*index=5*/bf16[8192,128]{1,0:T(8,128)(2,1)}, ...), branch_computations={%region_8.8_spmd, %region_9.9_spmd} | conditional | flops 203985152 | bytes 3295290 | solution.py:136
  205.1 1.4 fusion.30
  206.6 1.5 fusion.33
  208.6 0.6 copy-done.3
  209.2 35.9 %while.58 = (s32[]{:T(128)}, f32[256,128]{1,0:T(8,128)S(1)}, f32[256,128]{1,0:T(8,128)S(1)}, s32[]{:T(128)}, bf16[8192,128]{1,0:T(8,128)(2,1)}, /*index=5*/bf16[...) while((s32[]{:T(128)}, f32[256,128]{1,0:T(8,128)S(1)}, ...), condition=%wide.region_14.15_spmd.clone.clone, body=%wide.region_11.14_spmd.clone.clone.sunk | while | flops 270861568 | bytes 4887901 | solution.py:192
  209.2 4.4 %conditional.12 = ((f32[256,128]{1,0:T(8,128)S(1)}, f32[256,128]{1,0:T(8,128)S(1)})) conditional(s32[]{:T(128)} %convert_element_type.70, (f32[256,128]{1,0:T(8,128)S(1)}, f32[256,128]{1,0:T(8,128)S(1)}) %tuple.151, (s32[]{:T(128)}, s32[]{:T(128)}, bf16[8192,128]{1,0:T(8,128)(2,1)}, bf16[256,128]{1,0:T(8,128)(2,1)S(1)}, f32[8192]{0:T(1024)S(1)}, ...), branch_computations={%region_12.12_spmd, %region_13.13_spmd} | conditional | flops 270861568 | bytes 4886610 | solution.py:181
  209.2 1.4 fusion.50
  210.6 1.7 fusion.53
  212.3 1.3 convolution_add_fusion.1
  213.6 4.5 %conditional.12 = ((f32[256,128]{1,0:T(8,128)S(1)}, f32[256,128]{1,0:T(8,128)S(1)})) conditional(s32[]{:T(128)} %convert_element_type.70, (f32[256,128]{1,0:T(8,128)S(1)}, f32[256,128]{1,0:T(8,128)S(1)}) %tuple.151, (s32[]{:T(128)}, s32[]{:T(128)}, bf16[8192,128]{1,0:T(8,128)(2,1)}, bf16[256,128]{1,0:T(8,128)(2,1)S(1)}, f32[8192]{0:T(1024)S(1)}, ...), branch_computations={%region_12.12_spmd, %region_13.13_spmd} | conditional | flops 270861568 | bytes 4886610 | solution.py:181
  213.7 1.4 fusion.50
  215.1 1.7 fusion.53
  216.8 1.3 convolution_add_fusion.1
  218.1 4.5 %conditional.12 = ((f32[256,128]{1,0:T(8,128)S(1)}, f32[256,128]{1,0:T(8,128)S(1)})) conditional(s32[]{:T(128)} %convert_element_type.70, (f32[256,128]{1,0:T(8,128)S(1)}, f32[256,128]{1,0:T(8,128)S(1)}) %tuple.151, (s32[]{:T(128)}, s32[]{:T(128)}, bf16[8192,128]{1,0:T(8,128)(2,1)}, bf16[256,128]{1,0:T(8,128)(2,1)S(1)}, f32[8192]{0:T(1024)S(1)}, ...), branch_computations={%region_12.12_spmd, %region_13.13_spmd} | conditional | flops 270861568 | bytes 4886610 | solution.py:181
  218.2 1.4 fusion.50
  219.6 1.7 fusion.53
  221.3 1.3 convolution_add_fusion.1
  222.6 4.5 %conditional.12 = ((f32[256,128]{1,0:T(8,128)S(1)}, f32[256,128]{1,0:T(8,128)S(1)})) conditional(s32[]{:T(128)} %convert_element_type.70, (f32[256,128]{1,0:T(8,128)S(1)}, f32[256,128]{1,0:T(8,128)S(1)}) %tuple.151, (s32[]{:T(128)}, s32[]{:T(128)}, bf16[8192,128]{1,0:T(8,128)(2,1)}, bf16[256,128]{1,0:T(8,128)(2,1)S(1)}, f32[8192]{0:T(1024)S(1)}, ...), branch_computations={%region_12.12_spmd, %region_13.13_spmd} | conditional | flops 270861568 | bytes 4886610 | solution.py:181
  222.7 1.4 fusion.50
  224.1 1.7 fusion.53
  225.8 1.3 convolution_add_fusion.1
  227.1 4.5 %conditional.12 = ((f32[256,128]{1,0:T(8,128)S(1)}, f32[256,128]{1,0:T(8,128)S(1)})) conditional(s32[]{:T(128)} %convert_element_type.70, (f32[256,128]{1,0:T(8,128)S(1)}, f32[256,128]{1,0:T(8,128)S(1)}) %tuple.151, (s32[]{:T(128)}, s32[]{:T(128)}, bf16[8192,128]{1,0:T(8,128)(2,1)}, bf16[256,128]{1,0:T(8,128)(2,1)S(1)}, f32[8192]{0:T(1024)S(1)}, ...), branch_computations={%region_12.12_spmd, %region_13.13_spmd} | conditional | flops 270861568 | bytes 4886610 | solution.py:181
  227.2 1.4 fusion.50
  228.6 1.7 fusion.53
  230.3 1.3 convolution_add_fusion.1
  231.6 4.5 %conditional.12 = ((f32[256,128]{1,0:T(8,128)S(1)}, f32[256,128]{1,0:T(8,128)S(1)})) conditional(s32[]{:T(128)} %convert_element_type.70, (f32[256,128]{1,0:T(8,128)S(1)}, f32[256,128]{1,0:T(8,128)S(1)}) %tuple.151, (s32[]{:T(128)}, s32[]{:T(128)}, bf16[8192,128]{1,0:T(8,128)(2,1)}, bf16[256,128]{1,0:T(8,128)(2,1)S(1)}, f32[8192]{0:T(1024)S(1)}, ...), branch_computations={%region_12.12_spmd, %region_13.13_spmd} | conditional | flops 270861568 | bytes 4886610 | solution.py:181
  231.7 1.4 fusion.50
  233.1 1.7 fusion.53
  234.8 1.3 convolution_add_fusion.1
  236.1 4.5 %conditional.12 = ((f32[256,128]{1,0:T(8,128)S(1)}, f32[256,128]{1,0:T(8,128)S(1)})) conditional(s32[]{:T(128)} %convert_element_type.70, (f32[256,128]{1,0:T(8,128)S(1)}, f32[256,128]{1,0:T(8,128)S(1)}) %tuple.151, (s32[]{:T(128)}, s32[]{:T(128)}, bf16[8192,128]{1,0:T(8,128)(2,1)}, bf16[256,128]{1,0:T(8,128)(2,1)S(1)}, f32[8192]{0:T(1024)S(1)}, ...), branch_computations={%region_12.12_spmd, %region_13.13_spmd} | conditional | flops 270861568 | bytes 4886610 | solution.py:181
  236.2 1.4 fusion.50
  237.6 1.7 fusion.53
  239.3 1.3 convolution_add_fusion.1
  240.6 4.5 %conditional.12 = ((f32[256,128]{1,0:T(8,128)S(1)}, f32[256,128]{1,0:T(8,128)S(1)})) conditional(s32[]{:T(128)} %convert_element_type.70, (f32[256,128]{1,0:T(8,128)S(1)}, f32[256,128]{1,0:T(8,128)S(1)}) %tuple.151, (s32[]{:T(128)}, s32[]{:T(128)}, bf16[8192,128]{1,0:T(8,128)(2,1)}, bf16[256,128]{1,0:T(8,128)(2,1)S(1)}, f32[8192]{0:T(1024)S(1)}, ...), branch_computations={%region_12.12_spmd, %region_13.13_spmd} | conditional | flops 270861568 | bytes 4886610 | solution.py:181
  240.7 1.4 fusion.50
  242.1 1.7 fusion.53
  243.8 1.3 convolution_add_fusion.1
  245.1 0.6 copy-done.1
  245.8 0.0 copy-done.2
  (110 shorter events, 0.9 us)
Async XLA Ops:
  7.2 28.1 %copy-start = (bf16[32,1024]{1,0:T(8,128)(2,1)S(1)}, bf16[32,1024]{1,0:T(8,128)(2,1)}, u32[]{:S(2)}) copy-start(bf16[32,1024]{1,0:T(8,128)(2,1)} %param.18) | copy-start | bytes 196612
  7.2 111.7 %copy-start.5 = (bf16[256,128]{1,0:T(8,128)(2,1)S(1)}, bf16[256,128]{1,0:T(8,128)(2,1)}, u32[]{:S(2)}) copy-start(bf16[256,128]{1,0:T(8,128)(2,1)} %param.16) | copy-start | bytes 196612
  7.2 63.5 %copy-start.4 = (bf16[256,128]{1,0:T(8,128)(2,1)S(1)}, bf16[256,128]{1,0:T(8,128)(2,1)}, u32[]{:S(2)}) copy-start(bf16[256,128]{1,0:T(8,128)(2,1)} %param.19) | copy-start | bytes 196612
  7.2 76.8 %all-gather.7.cloned.1.call-start = ((), (), s32[]{:S(2)}) async-start(), calls=%async_computation.2 | async-start | bytes 2359296 | tf_op jit(solution)/shard_map/all_gather | solution.py:16
  35.2 83.6 %all-gather.9.cloned.1.call-start = ((), (), s32[]{:S(2)}) async-start(), calls=%async_computation.3 | async-start | bytes 2359296 | tf_op jit(solution)/shard_map/all_gather | solution.py:16
  56.3 152.3 %all-gather.11.cloned.1.call-start = ((), (), s32[]{:S(2)}) async-start(), calls=%async_computation.4 | async-start | bytes 2359296 | tf_op jit(solution)/shard_map/all_gather | solution.py:16
  70.7 137.9 %all-gather.13.cloned.1.call-start = ((), (), s32[]{:S(2)}) async-start(), calls=%async_computation.5 | async-start | bytes 2359296 | tf_op jit(solution)/shard_map/all_gather | solution.py:16
  208.5 0.7 copy-start.3
  245.1 0.7 copy-start.1
  245.1 0.7 copy-start.2
Sparse Core Ops, SparseCore 0:
  35.3 42.2 all-gather.6
  79.4 39.4 all-gather.8
  120.6 39.4 all-gather.10
  161.7 39.5 all-gather.12
